TPU v7x, 32 devices: a whole 2x2x4 slice. The times are simulated.
32 devices in a mesh: groups: 2 (over y), expert: 8 (over z, core), dp: 2 (over x).
Axes of the slice: x: 2, y: 2, z: 4, core: 2. Of those that a mesh axis runs over, the one named last changes fastest.
Arguments:
- tokens: bfloat16 [1024, 2048], P(('groups', 'expert'), 'dp'), parts along dimension 0, may hold values from -6 to 6
- expert_ids: int32 [1024, 8], P(('groups', 'expert')), parts along dimension 0, may hold values from 0 to 15, all different within a row; in each aligned block of 64 rows (0 to 63, 64 to 127, ...) at most 64 rows name the same one
- gate_levels: int32 [1024, 8], P(('groups', 'expert')), parts along dimension 0, may hold values from 1 to 255
- gate_weight: bfloat16 [16, 2048, 1536], P('expert', None, 'dp'), may hold values from -0.125 to 0.125
- up_weight: bfloat16 [16, 2048, 1536], P('expert', None, 'dp'), may hold values from -0.125 to 0.125
- down_weight: bfloat16 [16, 1536, 2048], P('expert', None, 'dp'), may hold values from -0.15625 to 0.15625
Outputs:
- mixed: bfloat16 [1024, 2048], P(('groups', 'expert'), 'dp'), parts along dimension 0
There are 2 independent parts, one for each index of `groups`. A program takes and returns all parts, laid end to end along the dimension named above; an argument that names none is the same for every part. Nothing has to cross between parts.
Inputs may be any that keep to these rules, and one draw needn't show every extreme that they name: `expert_ids`: each row names 8 different experts. Among the rows of one index of the expert axis no expert is named more than 64 times, a bound that some block reaches.
All inputs are finite; a program needn't handle non-finite values.
Results may differ from a plain program's by a relative error of at most 0.0057.
Values may be sent and summed in bfloat16 or wider, within the bound.
A program may use at most 64 MiB of HBM per device.

v0:
```python
import jax
import jax.numpy as jnp
from jax import lax
from jax.sharding import PartitionSpec as P


def slot_numbers(chosen_ids, experts, capacity):
    flat_ids = chosen_ids.reshape(-1)
    labels = jnp.arange(experts, dtype=jnp.int32)
    onehot = (flat_ids[:, None] == labels[None, :]).astype(jnp.int32)
    before = jnp.cumsum(onehot, axis=0) - onehot
    position = jnp.sum(before * onehot, axis=1)
    return (flat_ids * capacity + position).reshape(chosen_ids.shape)


def route_matrix(slots, count):
    targets = jnp.arange(count, dtype=jnp.int32)
    return jnp.any(targets[:, None, None] == slots[None, :, :], axis=2).astype(jnp.bfloat16)


def on_device(tokens, expert_ids, gate_levels, gate_weight, up_weight, down_weight):
    tok_dev = tokens.shape[0]
    picks = expert_ids.shape[1]
    exp_dev = gate_weight.shape[0]
    n_expert = lax.axis_size("expert")
    experts = exp_dev * n_expert
    capacity = min(tok_dev, max(2, 2 * tok_dev * picks // experts))
    slot_count = experts * capacity
    own_slots = slot_numbers(expert_ids, experts, capacity)
    route = route_matrix(own_slots, slot_count)
    whole = lax.all_gather(tokens, "dp", axis=1, tiled=True)
    outgoing = jnp.dot(route, whole, preferred_element_type=jnp.float32).astype(jnp.bfloat16)
    outgoing = outgoing.reshape(n_expert, exp_dev, capacity, whole.shape[1])
    arrived = lax.all_to_all(outgoing, "expert", split_axis=0, concat_axis=0, tiled=True)
    gate_part = jnp.einsum(
        "sxcd,xdf->sxcf", arrived, gate_weight, preferred_element_type=jnp.float32
    )
    up_part = jnp.einsum("sxcd,xdf->sxcf", arrived, up_weight, preferred_element_type=jnp.float32)
    hidden = (jax.nn.silu(gate_part) * up_part).astype(jnp.bfloat16)
    out_features = down_weight.shape[2]
    outputs = jnp.einsum(
        "sxcf,xfk->sxck",
        lax.all_gather(hidden, "dp", axis=3, tiled=True),
        down_weight,
        preferred_element_type=jnp.float32,
    )
    result = outputs.astype(jnp.bfloat16)
    returned = lax.all_to_all(result, "expert", split_axis=0, concat_axis=0, tiled=True)
    returned = returned.reshape(slot_count, out_features)
    shares = gate_levels.astype(jnp.float32) / 256.0
    targets = jnp.arange(slot_count, dtype=jnp.int32)
    weighting = jnp.sum(
        jnp.where(
            targets[None, :, None] == own_slots[:, None, :], shares[:, None, :], jnp.float32(0.0)
        ),
        axis=2,
    )
    weighting = weighting.astype(jnp.bfloat16)
    combined = jnp.dot(weighting, returned, preferred_element_type=jnp.float32)
    return combined.astype(jnp.bfloat16)


def solution(mesh):
    in_specs = (
        P(("groups", "expert"), "dp"),
        P(("groups", "expert"), None),
        P(("groups", "expert"), None),
        P("expert", None, "dp"),
        P("expert", None, "dp"),
        P("expert", None, "dp"),
    )
    out_specs = P(("groups", "expert"), "dp")
    return jax.shard_map(
        on_device, mesh=mesh, in_specs=in_specs, out_specs=out_specs, check_vma=False
    )
```

profile of v0, /device:TPU:0, one launch (start us, length us, event | category | flops | bytes accessed | tf_op | source)
XLA Modules:
  0.0 241.4 jit_solution(17744205040662272902)
XLA Ops:
  6.5 0.0 all-gather.2.cloned.1.call-start
  6.5 0.8 copy.37
  7.3 0.1 eq.56
  7.4 0.1 eq.52
  7.5 1.2 reduce-window.6
  8.7 0.2 slice_reduce_fusion
  8.9 0.1 fusion.22
  9.0 0.1 reduce_sum.21
  9.1 0.1 copy.40
  9.2 0.7 multiply_add_fusion
  9.9 0.1 copy.41
  10.0 0.7 fusion.12
  10.7 7.4 %all_gather.6 = bf16[64,2048]{1,0:T(8,128)(2,1)S(1)} all-gather(bf16[64,1024]{1,0:T(8,128)(2,1)} %param.6), channel_id=1, replica_groups=mesh['groups'=2,'expert'=8,'dp'=2] {'dp'}, dimensions={1}, use_global_device_ids=true | all-gather | bytes 393216 | tf_op jit(solution)/shard_map/all_gather | solution.py:31
  18.1 0.0 slice-start
  18.1 1.3 convolution_convert_fusion
  19.4 0.0 slice-start.1
  19.4 0.0 slice-start.2
  19.4 99.1 %all_to_all.10 = bf16[8,2,64,2048]{3,2,1,0:T(8,128)(2,1)S(1)} all-to-all(bf16[8,2,64,2048]{3,2,1,0:T(8,128)(2,1)S(1)} %bitcast.64), channel_id=1, replica_groups=mesh['groups'=2,'expert'=8,'dp'=2] {'expert'}, dimensions={0} | all-to-all | bytes 8388608 | tf_op jit(solution)/shard_map/all_to_all | solution.py:34
  118.5 0.0 slice-done
  118.5 0.0 slice-done.1
  118.5 0.0 slice-start.3
  118.5 3.5 %fusion.2 = f32[2,8,64,768]{3,2,1,0:T(8,128)S(1)} fusion(bf16[2,2048,768]{2,1,0:T(8,128)(2,1)S(1)} %bitcast.67, bf16[8,2,64,2048]{3,2,1,0:T(8,128)(2,1)S(1)} %all_to_all.10), kind=kOutput, calls=%fused_computation.2 | convolution fusion | flops 3221225472 | bytes 13631488 | tf_op jit(solution)/shard_map/sxcd,xdf->sxcf/dot_general | solution.py:38
  122.0 0.0 slice-done.2
  122.0 0.0 slice-done.3
  122.0 4.9 %fusion.8 = bf16[8,2,64,768]{3,2,0,1:T(8,128)(2,1)} fusion(f32[2,8,64,768]{3,2,1,0:T(8,128)S(1)} %fusion.2, bf16[2,2048,768]{2,1,0:T(8,128)(2,1)S(1)} %bitcast.69, bf16[8,2,64,2048]{3,2,1,0:T(8,128)(2,1)S(1)} %all_to_all.10), kind=kOutput, calls=%fused_computation.10 | convolution fusion | flops 3225944064 | bytes 15204352 | tf_op jit(solution)/shard_map/sxcd,xdf->sxcf/dot_general | solution.py:35
  126.9 0.0 all-gather.2.cloned.1.call-update
  126.9 44.0 %all-gather.2.cloned.1.call-done = bf16[8,2,64,1536]{3,2,0,1:T(8,128)(2,1)} async-done(((bf16[8,2,64,768]{3,2,0,1:T(8,128)(2,1)}), bf16[8,2,64,1536]{3,2,0,1:T(8,128)(2,1)}) %all-gather.2.cloned.1.call-update) | async-done | bytes 3145744 | tf_op jit(solution)/shard_map/all_gather | solution.py:43
  170.9 7.2 %convert_bitcast_fusion = bf16[8,2,64,1024]{3,2,0,1:T(8,128)(2,1)S(1)} fusion(bf16[8,2,64,1536]{3,2,0,1:T(8,128)(2,1)} %all-gather.2.cloned.1.call-done, bf16[2,1536,1024]{2,1,0:T(8,128)(2,1)} %param.11), kind=kOutput, calls=%fused_computation.16 | convolution fusion | flops 3222274048 | bytes 11534336 | tf_op jit(solution)/shard_map/sxcf,xfk->sxck/dot_general | solution.py:41
  178.1 1.6 copy.46
  179.6 0.0 copy-start
  179.6 4.7 %all-to-all-start.1 = ((bf16[8,2,64,1024]{3,2,1,0:T(8,128)(2,1)}), bf16[8,2,64,1024]{3,2,1,0:T(8,128)(2,1)S(1)}, u32[]{:S(2)}, u32[]{:S(2)}) async-start(bf16[8,2,64,1024]{3,2,1,0:T(8,128)(2,1)} %copy.46), calls=%async_computation.1 | async-start | bytes 4194304 | tf_op jit(solution)/shard_map/all_to_all | solution.py:48
  184.4 0.0 copy-done
  184.4 0.1 copy.42
  184.5 0.7 select_reduce_fusion
  185.2 48.2 %all-to-all-done.1 = bf16[8,2,64,1024]{3,2,1,0:T(8,128)(2,1)S(1)} async-done(((bf16[8,2,64,1024]{3,2,1,0:T(8,128)(2,1)}), bf16[8,2,64,1024]{3,2,1,0:T(8,128)(2,1)S(1)}, u32[]{:S(2)}, u32[]{:S(2)}) %all-to-all-start.1) | async-done | bytes 2097184 | tf_op jit(solution)/shard_map/all_to_all | solution.py:48
  233.4 1.1 convolution_convert_fusion.1
  (6 shorter events, 0.1 us)
Async XLA Ops:
  6.5 164.4 %all-gather.2.cloned.1.call-start = ((), (), s32[]{:S(2)}) async-start(), calls=%async_computation.2 | async-start | bytes 4718592 | tf_op jit(solution)/shard_map/all_gather | solution.py:43
  18.1 100.4 %slice-start = ((s8[6291456]{0:T(1024)(128)(4,1)}), s8[4194304]{0:T(1024)(128)(4,1)S(1)}, s32[]{:S(2)}) async-start(s8[6291456]{0:T(1024)(128)(4,1)} %bitcast.66), calls=%async_computation.3 | async-start | bytes 8388608
  19.4 99.1 %slice-start.1 = ((s8[6291456]{0:T(1024)(128)(4,1)}), s8[2097152]{0:T(1024)(128)(4,1)S(1)}, s32[]{:S(2)}) async-start(s8[6291456]{0:T(1024)(128)(4,1)} %bitcast.66), calls=%async_computation.4 | async-start | bytes 4194304
  19.4 102.6 %slice-start.2 = ((s8[6291456]{0:T(1024)(128)(4,1)}), s8[4194304]{0:T(1024)(128)(4,1)S(1)}, s32[]{:S(2)}) async-start(s8[6291456]{0:T(1024)(128)(4,1)} %bitcast.68), calls=%async_computation.5 | async-start | bytes 8388608
  118.5 3.5 %slice-start.3 = ((s8[6291456]{0:T(1024)(128)(4,1)}), s8[2097152]{0:T(1024)(128)(4,1)S(1)}, s32[]{:S(2)}) async-start(s8[6291456]{0:T(1024)(128)(4,1)} %bitcast.68), calls=%async_computation.6 | async-start | bytes 4194304
  179.6 4.7 %copy-start = (s32[64,8]{0,1:T(8,128)S(1)}, s32[64,8]{0,1:T(8,128)}, u32[]{:S(2)}) copy-start(s32[64,8]{0,1:T(8,128)} %param.8) | copy-start | bytes 6148
  179.6 53.8 %all-to-all-start.1 = ((bf16[8,2,64,1024]{3,2,1,0:T(8,128)(2,1)}), bf16[8,2,64,1024]{3,2,1,0:T(8,128)(2,1)S(1)}, u32[]{:S(2)}, u32[]{:S(2)}) async-start(bf16[8,2,64,1024]{3,2,1,0:T(8,128)(2,1)} %copy.46), calls=%async_computation.1 | async-start | bytes 4194304 | tf_op jit(solution)/shard_map/all_to_all | solution.py:48
Sparse Core Ops, SparseCore 0:
  127.0 43.8 all-gather.1
where the time goes:
time: 242 us; the launch traced here: 241 us
  blocking collectives  107 us (44%)
  waiting for transfers between devices  92.2 us (38%)
  matrix products  17.9 us (7%)
  between operations  13.5 us (6%)
  starting transfers between devices  4.74 us (2%)
  other arithmetic  3.42 us (1%)
  local copies, waits for them, and re-layouts  3.08 us (1%)
    all_to_all x1, blocking collectives, on_device(): lax.all_to_all(outgoing, 'expert', split_axis=0, concat_axis=0, tiled=True)  99.1 us
    all_to_all x1, waiting for transfers between devices, on_device(): lax.all_to_all(result, 'expert', split_axis=0, concat_axis=0, tiled=True)  48.2 us
    all_gather x1, waiting for transfers between devices, on_device(): lax.all_gather(hidden, 'dp', axis=3, tiled=True)  44 us
    all_gather x1, blocking collectives, on_device(): whole = lax.all_gather(tokens, 'dp', axis=1, tiled=True)  7.39 us
    dot_general x1, matrix products, on_device(): jnp.einsum('sxcf,xfk->sxck', lax.all_gather(hidden, 'dp', axis=3, tiled=T...  7.15 us
    dot_general x1, matrix products, on_device(): jnp.einsum('sxcd,xdf->sxcf', arrived, gate_weight, preferred_element_type...  4.87 us
  transfers between devices with their start and end apart: 2, of which 2 were waited for; matrix products, arithmetic and copies ran while one was open for 0% of the time, Pallas kernels for 0%

commit v1 on v0

--- a/solution.py
+++ b/solution.py
@@ -2,6 +2,18 @@
 import jax.numpy as jnp
 from jax import lax
 from jax.sharding import PartitionSpec as P
+
+
+def ring_product(value, axis, dim, term):
+    size, index = (lax.axis_size(axis), lax.axis_index(axis))
+    left = [(i, (i - 1) % size) for i in range(size)]
+    rows = value.shape[dim]
+    held = value
+    total = term(held, index * rows)
+    for step in range(1, size):
+        held = lax.ppermute(held, axis, left)
+        total = total + term(held, (index + step) % size * rows)
+    return total
 
 
 def slot_numbers(chosen_ids, experts, capacity):
@@ -38,11 +50,16 @@
     up_part = jnp.einsum("sxcd,xdf->sxcf", arrived, up_weight, preferred_element_type=jnp.float32)
     hidden = (jax.nn.silu(gate_part) * up_part).astype(jnp.bfloat16)
     out_features = down_weight.shape[2]
-    outputs = jnp.einsum(
-        "sxcf,xfk->sxck",
-        lax.all_gather(hidden, "dp", axis=3, tiled=True),
-        down_weight,
-        preferred_element_type=jnp.float32,
+    outputs = ring_product(
+        hidden,
+        "dp",
+        3,
+        lambda own_block, offset: jnp.einsum(
+            "sxcf,xfk->sxck",
+            own_block,
+            lax.dynamic_slice_in_dim(down_weight, offset, own_block.shape[3], axis=1),
+            preferred_element_type=jnp.float32,
+        ),
     )
     result = outputs.astype(jnp.bfloat16)
     returned = lax.all_to_all(result, "expert", split_axis=0, concat_axis=0, tiled=True)

time: 242 us -> 215 us (0.89)
  waiting for transfers between devices: 92.2 us -> 78.7 us
  between operations: 13.5 us -> 0.14 us
    all_gather x1 -> x0, waiting for transfers between devices: 44 us -> none  [on_device(): lax.all_gather(hidden, 'dp', axis=3, tiled=True)]
    ppermute x0 -> x1, waiting for transfers between devices: none -> 30.6 us  [ring_product(): held = lax.ppermute(held, axis, left)]
    dot_general x1 -> x2, matrix products: 7.15 us -> 7.41 us  [on_device(): jnp.einsum('sxcf,xfk->sxck', own_block, lax.dynamic_slice_in_dim(down_wei...]
  transfers between devices with their start and end apart: 2 -> 2, of which waited for: 2 -> 2; matrix products, arithmetic and copies ran while one was open for 0% -> 2% of each run, Pallas kernels for 0% -> 0%
where the time goes in v1:
time: 215 us; the launch traced here: 214 us
  blocking collectives  107 us (50%)
  waiting for transfers between devices  78.7 us (37%)
  matrix products  17.2 us (8%)
  starting transfers between devices  5.29 us (2%)
  other arithmetic  3.42 us (2%)
  local copies, waits for them, and re-layouts  3.09 us (1%)
    all_to_all x1, blocking collectives, on_device(): lax.all_to_all(outgoing, 'expert', split_axis=0, concat_axis=0, tiled=True)  99.1 us
    all_to_all x1, waiting for transfers between devices, on_device(): lax.all_to_all(result, 'expert', split_axis=0, concat_axis=0, tiled=True)  48.1 us
    ppermute x1, waiting for transfers between devices, ring_product(): held = lax.ppermute(held, axis, left)  30.6 us
    dot_general x2, matrix products, on_device(): jnp.einsum('sxcf,xfk->sxck', own_block, lax.dynamic_slice_in_dim(down_wei...  7.41 us
    all_gather x1, blocking collectives, on_device(): whole = lax.all_gather(tokens, 'dp', axis=1, tiled=True)  7.39 us
  transfers between devices with their start and end apart: 2, of which 2 were waited for; matrix products, arithmetic and copies ran while one was open for 2% of the time, Pallas kernels for 0%

profile of v1, /device:TPU:0, one launch (start us, length us, event | category | flops | bytes accessed | tf_op | source)
XLA Modules:
  0.0 214.3 jit_solution(309224287259834791)
XLA Ops:
  0.0 0.8 copy.37
  0.8 0.1 eq.54
  0.9 0.1 eq.58
  1.0 1.2 reduce-window.6
  2.1 0.2 slice_reduce_fusion
  2.4 0.1 fusion.27
  2.5 0.1 reduce_sum.21
  2.6 0.1 copy.40
  2.6 0.7 multiply_add_fusion
  3.3 0.1 copy.41
  3.4 0.7 fusion.17
  4.1 7.4 %all_gather.3 = bf16[64,2048]{1,0:T(8,128)(2,1)S(1)} all-gather(bf16[64,1024]{1,0:T(8,128)(2,1)} %param.6), channel_id=1, replica_groups=mesh['groups'=2,'expert'=8,'dp'=2] {'dp'}, dimensions={1}, use_global_device_ids=true | all-gather | bytes 393216 | tf_op jit(solution)/shard_map/all_gather | solution.py:43
  11.5 0.0 slice-start
  11.5 1.3 convolution_convert_fusion
  12.8 0.0 slice-start.1
  12.8 0.0 slice-start.2
  12.9 99.1 %all_to_all.10 = bf16[8,2,64,2048]{3,2,1,0:T(8,128)(2,1)S(1)} all-to-all(bf16[8,2,64,2048]{3,2,1,0:T(8,128)(2,1)S(1)} %bitcast.70), channel_id=1, replica_groups=mesh['groups'=2,'expert'=8,'dp'=2] {'expert'}, dimensions={0} | all-to-all | bytes 8388608 | tf_op jit(solution)/shard_map/all_to_all | solution.py:46
  112.0 0.0 slice-done
  112.0 0.0 slice-done.1
  112.0 0.0 slice-start.3
  112.0 3.5 %fusion = f32[2,8,64,768]{3,2,1,0:T(8,128)S(1)} fusion(bf16[2,2048,768]{2,1,0:T(8,128)(2,1)S(1)} %bitcast.73, bf16[8,2,64,2048]{3,2,1,0:T(8,128)(2,1)S(1)} %all_to_all.10), kind=kOutput, calls=%fused_computation | convolution fusion | flops 3221225472 | bytes 13631488 | tf_op jit(solution)/shard_map/sxcd,xdf->sxcf/dot_general | solution.py:50
  115.5 0.0 slice-done.2
  115.5 0.0 slice-done.3
  115.5 3.9 %fusion.10 = bf16[8,2,64,768]{3,2,0,1:T(8,128)(2,1)S(1)} fusion(f32[2,8,64,768]{3,2,1,0:T(8,128)S(1)} %fusion, bf16[2,2048,768]{2,1,0:T(8,128)(2,1)S(1)} %bitcast.75, bf16[8,2,64,2048]{3,2,1,0:T(8,128)(2,1)S(1)} %all_to_all.10), kind=kOutput, calls=%fused_computation.13 | convolution fusion | flops 3225944064 | bytes 15204352 | tf_op jit(solution)/shard_map/sxcd,xdf->sxcf/dot_general | solution.py:47
  119.3 1.6 collective-permute-start
  120.9 3.7 %fusion.8 = f32[2,1024,8,64]{1,3,2,0:T(8,128)S(1)} fusion(bf16[8,2,64,768]{3,2,0,1:T(8,128)(2,1)S(1)} %fusion.10, bf16[2,1536,1024]{2,1,0:T(8,128)(2,1)} %param.11, s32[]{:T(128)S(6)} %select_n.18), kind=kOutput, calls=%fused_computation.10 | convolution fusion | flops 1610612736 | bytes 8912900 | tf_op jit(solution)/shard_map/sxcf,xfk->sxck/dot_general | solution.py:57
  124.6 30.6 %collective-permute-done = bf16[8,2,64,768]{3,2,0,1:T(8,128)(2,1)S(1)} collective-permute-done((bf16[8,2,64,768]{3,2,0,1:T(8,128)(2,1)S(1)}, bf16[8,2,64,768]{3,2,0,1:T(8,128)(2,1)S(1)}, u32[]{:S(2)}, u32[]{:S(2)}) %collective-permute-start) | collective-permute-done | bytes 1572896 | tf_op jit(solution)/shard_map/ppermute | solution.py:14
  155.2 3.7 %fusion.16 = bf16[8,2,64,1024]{3,2,0,1:T(8,128)(2,1)S(1)} fusion(f32[2,1024,8,64]{1,3,2,0:T(8,128)S(1)} %fusion.8, bf16[8,2,64,768]{3,2,0,1:T(8,128)(2,1)S(1)} %collective-permute-done, bf16[2,1536,1024]{2,1,0:T(8,128)(2,1)} %param.11, s32[]{:T(128)S(6)} %select_n.20), kind=kOutput, calls=%fused_computation.21 | convolution fusion | flops 1612709888 | bytes 11010052 | tf_op jit(solution)/shard_map/sxcf,xfk->sxck/dot_general | solution.py:57
  158.9 1.6 copy.46
  160.5 0.0 copy-start
  160.5 3.7 %all-to-all-start.1 = ((bf16[8,2,64,1024]{3,2,1,0:T(8,128)(2,1)}), bf16[8,2,64,1024]{3,2,1,0:T(8,128)(2,1)S(1)}, u32[]{:S(2)}, u32[]{:S(2)}) async-start(bf16[8,2,64,1024]{3,2,1,0:T(8,128)(2,1)} %copy.46), calls=%async_computation.1 | async-start | bytes 4194304 | tf_op jit(solution)/shard_map/all_to_all | solution.py:65
  164.2 0.0 copy-done
  164.3 0.1 copy.42
  164.3 0.7 select_reduce_fusion
  165.1 48.1 %all-to-all-done.1 = bf16[8,2,64,1024]{3,2,1,0:T(8,128)(2,1)S(1)} async-done(((bf16[8,2,64,1024]{3,2,1,0:T(8,128)(2,1)}), bf16[8,2,64,1024]{3,2,1,0:T(8,128)(2,1)S(1)}, u32[]{:S(2)}, u32[]{:S(2)}) %all-to-all-start.1) | async-done | bytes 2097184 | tf_op jit(solution)/shard_map/all_to_all | solution.py:65
  213.2 1.1 convolution_convert_fusion.1
  (6 shorter events, 0.1 us)
Async XLA Ops:
  11.5 100.4 %slice-start = ((s8[6291456]{0:T(1024)(128)(4,1)}), s8[4194304]{0:T(1024)(128)(4,1)S(1)}, s32[]{:S(2)}) async-start(s8[6291456]{0:T(1024)(128)(4,1)} %bitcast.72), calls=%async_computation.2 | async-start | bytes 8388608
  12.8 99.1 %slice-start.1 = ((s8[6291456]{0:T(1024)(128)(4,1)}), s8[2097152]{0:T(1024)(128)(4,1)S(1)}, s32[]{:S(2)}) async-start(s8[6291456]{0:T(1024)(128)(4,1)} %bitcast.72), calls=%async_computation.3 | async-start | bytes 4194304
  12.8 102.6 %slice-start.2 = ((s8[6291456]{0:T(1024)(128)(4,1)}), s8[4194304]{0:T(1024)(128)(4,1)S(1)}, s32[]{:S(2)}) async-start(s8[6291456]{0:T(1024)(128)(4,1)} %bitcast.74), calls=%async_computation.4 | async-start | bytes 8388608
  112.0 3.5 %slice-start.3 = ((s8[6291456]{0:T(1024)(128)(4,1)}), s8[2097152]{0:T(1024)(128)(4,1)S(1)}, s32[]{:S(2)}) async-start(s8[6291456]{0:T(1024)(128)(4,1)} %bitcast.74), calls=%async_computation.5 | async-start | bytes 4194304
  119.3 35.8 %collective-permute-start = (bf16[8,2,64,768]{3,2,0,1:T(8,128)(2,1)S(1)}, bf16[8,2,64,768]{3,2,0,1:T(8,128)(2,1)S(1)}, u32[]{:S(2)}, u32[]{:S(2)}) collective-permute-start(bf16[8,2,64,768]{3,2,0,1:T(8,128)(2,1)S(1)} %fusion.10), channel_id=1, source_target_pairs={{0,1},{1,0},{2,3},{3,2},{4,5},{5,4},{6,7},{7,6},{8,9},{9,8},{10,11... | collective-permute-start | bytes 4718600 | tf_op jit(solution)/shard_map/ppermute | solution.py:14
  160.5 3.7 %copy-start = (s32[64,8]{0,1:T(8,128)S(1)}, s32[64,8]{0,1:T(8,128)}, u32[]{:S(2)}) copy-start(s32[64,8]{0,1:T(8,128)} %param.8) | copy-start | bytes 6148
  160.5 52.7 %all-to-all-start.1 = ((bf16[8,2,64,1024]{3,2,1,0:T(8,128)(2,1)}), bf16[8,2,64,1024]{3,2,1,0:T(8,128)(2,1)S(1)}, u32[]{:S(2)}, u32[]{:S(2)}) async-start(bf16[8,2,64,1024]{3,2,1,0:T(8,128)(2,1)} %copy.46), calls=%async_computation.1 | async-start | bytes 4194304 | tf_op jit(solution)/shard_map/all_to_all | solution.py:65
